TPU v7x, 32 devices: a whole 2x2x4 slice. The times are simulated.
32 devices in a mesh: light: 4 (over y, x), screen: 8 (over z, core).
Axes of the slice: x: 2, y: 2, z: 4, core: 2. Of those that a mesh axis runs over, the one named last changes fastest.
Arguments:
- density: float32 [128, 256, 512], P('screen', None, 'light'), may hold values from 0 to 1.09375, as said below
- albedo: float32 [128, 256, 512], P('screen', None, 'light'), may hold values from 0.2 to 1
- light_in: float32 [128, 256], replicated, may hold values from 0.5 to 1.5
- occupancy: int32 [8, 16, 32], P('screen', None, 'light'), may hold values 0 or 1
- phase: int32 [256, 512], replicated, may hold values from 0 to 15
- fractions: float32 [3, 16], replicated, may hold values from 0 to 1
Outputs:
- image: float32 [256, 512], P('screen', 'light')
- transmittance: float32 [256, 512], P('screen', 'light')
- lit_bricks: float32 [128, 256, 512], P('light', 'screen')
Inputs may be any that keep to these rules, and one draw needn't show every extreme that they name: `density`: nonnegative extinction of each cell. `occupancy`: 1 where the brick of 16 cells on a side is occupied.
All inputs are finite; a program needn't handle non-finite values. No bound on the sum of `occupancy` on one device may be relied on, other than what follows from the above.
Results may differ from a plain program's by a relative error of at most 0.0003.
Values sent between devices are 32-bit elements; how exact they have to be, the bound alone decides.
No kernel may reach another device: no remote copies, remote signals or barrier semaphores. Data moves between devices by JAX's collectives and lax.ppermute only.
A program may use at most 192 MiB of HBM per device.

v0:
```python
import jax
import jax.numpy as jnp
from jax import lax
from jax.sharding import PartitionSpec as P

BRICK = 16


def passed_along(value, axis, by):
    peers = lax.axis_size(axis)
    pairs = [(i, i + by) for i in range(peers) if 0 <= i + by < peers]
    return lax.ppermute(value, axis, pairs)


def carried_in(part, axis, combine, identity):
    place = lax.axis_index(axis)
    gathered = lax.all_gather(part, axis)
    state = jnp.zeros_like(part) + jnp.asarray(identity, part.dtype)

    def one(step, state):
        return combine(state, lax.dynamic_index_in_dim(gathered, step, 0, False))

    return lax.fori_loop(0, place, one, state)


def prefix_last(values):
    length = values.shape[-1]
    block = 128
    count = length // block
    shaped = values.reshape(values.shape[:-1] + (count, block))
    rowsidx = lax.broadcasted_iota(jnp.int32, (block, block), 0)
    colsidx = lax.broadcasted_iota(jnp.int32, (block, block), 1)
    upper = (rowsidx < colsidx).astype(jnp.float32)
    within = jnp.matmul(shaped, upper, precision=lax.Precision.HIGHEST)
    totals = jnp.sum(shaped, axis=-1)
    carried = jnp.cumsum(totals, axis=-1) - totals
    return (within + carried[..., None]).reshape(values.shape)


def prefix_first(values):
    length = values.shape[0]
    count = length // length
    shaped = values.reshape(count, length, -1)
    rowsidx = lax.broadcasted_iota(jnp.int32, (length, length), 0)
    colsidx = lax.broadcasted_iota(jnp.int32, (length, length), 1)
    lower = (colsidx < rowsidx).astype(jnp.float32)
    within = jnp.einsum("ij,bjr->bir", lower, shaped, precision=lax.Precision.HIGHEST)
    totals = jnp.sum(shaped, axis=1)
    carried = jnp.cumsum(totals, axis=0) - totals
    return (within + carried[:, None]).reshape(values.shape)


def corner_fractions(rays, fractions):
    levels = lax.broadcasted_iota(jnp.int32, (fractions.shape[1], 1, 1), 0)
    onehot = (rays[None] == levels).astype(jnp.float32)
    return jnp.einsum("kp,prc->krc", fractions, onehot, precision=lax.Precision.HIGHEST)


def resample(field, tail, weights, deep, cols):
    first = field[:, 0:cols]
    second = field[:, 1 : cols + 1]
    edge_first = tail[:, 0:cols]
    edge_second = tail[:, 1 : cols + 1]
    first_next = jnp.concatenate([first[:, :, 1:], edge_first], axis=2)
    second_next = jnp.concatenate([second[:, :, 1:], edge_second], axis=2)
    depth_w = weights[0]
    column_w = weights[1]
    light_w = weights[2]
    near = first + column_w * (second - first)
    further = first_next + column_w * (second_next - first_next)
    mixed = near + light_w * (further - near)
    lower = mixed[0:deep]
    higher = mixed[1 : deep + 1]
    return lower + depth_w * (higher - lower)


def composite(extinct, shaded):
    screened = prefix_first(extinct)
    part = jnp.sum(jnp.exp(-screened) * (1.0 - jnp.exp(-extinct)) * shaded, axis=0)
    return (part, jnp.sum(extinct, axis=0))


def finish(parts, totals):
    before = jnp.cumsum(totals, axis=0) - totals
    picture = jnp.sum(jnp.exp(-before) * parts, axis=0)
    return (picture, jnp.exp(-jnp.sum(totals, axis=0)))


def march_slabs(masked, lit, phase, fractions):
    slab_b, width_a, slab_l = masked.shape
    light_idx = lax.axis_index("light")
    rims = passed_along((masked[:2], lit[:2]), "screen", -1)
    dens_ext = jnp.pad(jnp.concatenate([masked, rims[0]], axis=0), ((0, 0), (0, 2), (0, 0)))
    lit_ext = jnp.pad(jnp.concatenate([lit, rims[1]], axis=0), ((0, 0), (0, 2), (0, 0)))
    tails = passed_along((dens_ext[:, :, :1], lit_ext[:, :, :1]), "light", -1)
    rays = lax.dynamic_slice_in_dim(phase, light_idx * slab_l, slab_l, 1)
    weights = corner_fractions(rays, fractions)
    extinct = resample(dens_ext, tails[0], weights, slab_b, width_a)
    shaded = resample(lit_ext, tails[1], weights, slab_b, width_a)
    part, total = composite(extinct, shaded)
    parts, totals = (
        lax.all_to_all(part[None], "screen", split_axis=1, concat_axis=0, tiled=True),
        lax.all_to_all(total[None], "screen", split_axis=1, concat_axis=0, tiled=True),
    )
    return finish(parts, totals)


def local(density, albedo, light_in, occupancy, phase, fractions):
    slab_b, width_a, slab_l = density.shape
    bricks_b, bricks_a, bricks_l = occupancy.shape
    masked = (
        density.reshape(bricks_b, BRICK, bricks_a, BRICK, bricks_l, BRICK)
        * occupancy.astype(jnp.float32)[:, None, :, None, :, None]
    ).reshape(density.shape)
    screen_idx = lax.axis_index("screen")
    local_depth = prefix_last(masked)
    totals = jnp.sum(masked, axis=2)
    before = carried_in(totals, "light", jnp.add, jnp.zeros_like(totals))
    incoming = lax.dynamic_slice_in_dim(light_in, screen_idx * slab_b, slab_b, 0)
    lit = albedo * incoming[:, :, None] * jnp.exp(-(local_depth + before[:, :, None]))
    lit_cam = lax.all_to_all(lit, "screen", split_axis=1, concat_axis=0, tiled=True)
    lit_cam = lax.all_to_all(lit_cam, "light", split_axis=0, concat_axis=2, tiled=True)
    picture, passing = march_slabs(masked, lit, phase, fractions)
    return (picture, passing, lit_cam)


def solution(mesh):
    return jax.shard_map(
        local,
        mesh=mesh,
        in_specs=(
            P("screen", None, "light"),
            P("screen", None, "light"),
            P(),
            P("screen", None, "light"),
            P(),
            P(),
        ),
        out_specs=(P("screen", "light"), P("screen", "light"), P("light", "screen", None)),
        check_vma=False,
    )
```

profile of v0, /device:TPU:0, one launch (start us, length us, event | category | flops | bytes accessed | tf_op | source)
XLA Modules:
  0.0 195.5 jit_solution(17380704200879934052)
XLA Ops:
  1.9 2.2 %fusion.35 = (f32[16,256]{1,0:T(8,128)S(1)}, f32[16,256,128]{2,1,0:T(8,128)S(1)}) fusion(f32[16,256,128]{2,1,0:T(8,128)} %param.8, f32[256,128]{1,0:T(8,128)S(1)} %mul.121), kind=kLoop, calls=%fused_computation.62 | loop fusion | flops 1044480 | bytes 4341760 | tf_op jit(solution)/shard_map/reduce_sum | solution.py:35
  4.2 9.7 %all-gather = f32[64,256]{1,0:T(8,128)S(1)} all-gather(f32[16,256]{1,0:T(8,128)S(1)} %get-tuple-element.35), channel_id=2, replica_groups=mesh['light'=4,'screen'=8] {'light'}, dimensions={0}, use_global_device_ids=true | all-gather | bytes 81920 | tf_op jit(solution)/shard_map/all_gather | solution.py:17
  14.6 3.8 %exponential_multiply_fusion = f32[16,256,128]{2,1,0:T(8,128)S(1)} fusion(f32[16,256,128]{2,1,0:T(8,128)} %param.9, f32[16,256,128]{2,1,0:T(8,128)S(1)} %get-tuple-element.36, f32[16,256]{1,0:T(8,128)S(1)} %get-tuple-element.26, f32[16,256]{1,0:T(8,128)S(1)} %sub.66, f32[16,256]{1,0:T(8,128)S(1)} %constant_dynamic-slice_fusion), kind=kOutput, calls=%fused_computation.42 | convolution fusion | flops 807944192 | bytes 6340608 | tf_op jit(solution)/shard_map/dot_general | solution.py:34
  21.1 10.6 %reshape.82 = f32[1,16,16,16,8,16]{5,4,3,2,1,0:T(8,128)} reshape(f32[16,256,128]{2,1,0:T(8,128)} %param.8) | data formatting | bytes 4194304 | tf_op jit(solution)/shard_map/reshape | solution.py:112
  31.7 1.9 slice_multiply_fusion
  37.9 1.7 pad_maximum_fusion.1
  39.6 2.1 %pad_slice_fusion.2 = f32[18,256,127]{2,1,0:T(8,128)} fusion(f32[18,256,128]{2,1,0:T(8,128)S(1)} %pad_maximum_fusion.1), kind=kLoop, calls=%fused_computation.25 | loop fusion | bytes 4700160 | tf_op jit(solution)/shard_map/slice | solution.py:65
  41.7 1.6 pad_slice_fusion.3
  44.4 2.2 %pad_slice_fusion.4 = f32[18,256,127]{2,1,0:T(8,128)} fusion(f32[18,256,128]{2,1,0:T(8,128)S(1)} %pad_maximum_fusion), kind=kLoop, calls=%fused_computation.27 | loop fusion | bytes 4700160 | tf_op jit(solution)/shard_map/slice | solution.py:65
  46.6 1.6 pad_slice_fusion.5
  48.2 2.7 %copy.33 = f32[18,258,1]{1,2,0:T(1,128)S(1)} copy(f32[18,258,1]{2,1,0:T(8,128)} %pad_slice_fusion.3) | data formatting | bytes 37152 | tf_op jit(solution)/shard_map/slice | solution.py:95
  52.2 2.7 %copy.30 = f32[18,258,1]{1,2,0:T(1,128)S(1)} copy(f32[18,258,1]{2,1,0:T(8,128)} %pad_slice_fusion.5) | data formatting | bytes 37152 | tf_op jit(solution)/shard_map/slice | solution.py:95
  56.5 3.7 %fusion.3 = f32[18,256,127]{2,1,0:T(8,128)} fusion(f32[2,256,128]{2,1,0:T(8,128)S(1)} %collective-permute-done.2, f32[16,256,128]{2,1,0:T(8,128)} %copy-done.3), kind=kLoop, calls=%fused_computation.9 | loop fusion | flops 585216 | bytes 4700160 | tf_op jit(solution)/shard_map/concatenate | solution.py:94
  60.2 2.1 %fusion.4 = f32[18,256,127]{2,1,0:T(8,128)} fusion(f32[2,256,128]{2,1,0:T(8,128)S(1)} %collective-permute-done, f32[16,256,128]{2,1,0:T(8,128)S(1)} %copy-done.7), kind=kLoop, calls=%fused_computation.10 | loop fusion | flops 585216 | bytes 4700160 | tf_op jit(solution)/shard_map/concatenate | solution.py:93
  62.4 2.1 %copy.35 = f32[18,256,1]{2,1,0:T(8,128)} copy(f32[18,256,1]{1,2,0:T(1,128)S(1)} %get-tuple-element.44) | data formatting | bytes 36864 | tf_op jit(solution)/shard_map/slice | solution.py:63
  64.6 2.2 %copy.34 = f32[18,256,1]{2,1,0:T(8,128)} copy(f32[18,256,1]{1,2,0:T(1,128)S(1)} %get-tuple-element.45) | data formatting | bytes 36864 | tf_op jit(solution)/shard_map/slice | solution.py:62
  66.8 2.1 %copy.32 = f32[18,256,1]{2,1,0:T(8,128)} copy(f32[18,256,1]{1,2,0:T(1,128)S(1)} %get-tuple-element.46) | data formatting | bytes 36864 | tf_op jit(solution)/shard_map/slice | solution.py:63
  69.0 2.1 %copy.31 = f32[18,256,1]{2,1,0:T(8,128)} copy(f32[18,256,1]{1,2,0:T(1,128)S(1)} %get-tuple-element.47) | data formatting | bytes 36864 | tf_op jit(solution)/shard_map/slice | solution.py:62
  71.1 12.0 %fusion.14 = (f32[18,256,128]{2,1,0:T(8,128)}, f32[18,256,128]{2,1,0:T(8,128)S(1)}) fusion(f32[18,256,1]{2,1,0:T(8,128)} %copy.34, f32[18,256,127]{2,1,0:T(8,128)} %fusion.3, f32[18,256,1]{2,1,0:T(8,128)} %copy.35, f32[18,256,127]{2,1,0:T(8,128)} %pad_slice_fusion.2, f32[18,256,128]{2,1,0:T(8,128)S(1)} %pad_maximum_fusion.1, f32[256,128]{1,0:T(8,128)S(1)} %bitcast.74, ...), kind=kLoop, calls=%fused_computation.24 | loop fusion | flops 12976128 | bytes 19136512 | tf_op jit(solution)/shard_map/add | solution.py:71
  83.2 2.3 %fusion.36 = (f32[256,128]{1,0:T(8,128)}, f32[16,256,128]{2,1,0:T(8,128)}) fusion(f32[18,256,128]{2,1,0:T(8,128)S(1)} %get-tuple-element.43, f32[256,128]{1,0:T(8,128)S(1)} %bitcast.72), kind=kLoop, calls=%fused_computation.63 | loop fusion | flops 2064384 | bytes 6553600 | tf_op jit(solution)/shard_map/reduce_sum | solution.py:80
  85.5 6.7 %all-to-all-start = ((f32[1,256,128]{2,0,1:T(1,128)}), f32[1,256,128]{2,0,1:T(1,128)S(1)}, u32[]{:S(2)}, u32[]{:S(2)}) async-start(f32[1,256,128]{2,0,1:T(1,128)} %bitcast.7), calls=%async_computation | async-start | bytes 262144 | tf_op jit(solution)/shard_map/all_to_all | solution.py:103
  92.2 2.5 %copy.36 = f32[16,256,128]{2,0,1:T(8,128)} copy(f32[16,256,128]{2,1,0:T(8,128)S(1)} %copy-done.4) | data formatting | bytes 4194304 | tf_op jit(solution)/shard_map/mul | solution.py:120
  94.7 4.2 %all-to-all-done = f32[1,256,128]{2,0,1:T(1,128)S(1)} async-done(((f32[1,256,128]{2,0,1:T(1,128)}), f32[1,256,128]{2,0,1:T(1,128)S(1)}, u32[]{:S(2)}, u32[]{:S(2)}) %all-to-all-start) | async-done | bytes 131104 | tf_op jit(solution)/shard_map/all_to_all | solution.py:103
  98.9 4.4 %all-to-all-start.2 = ((f32[16,256,128]{2,0,1:T(8,128)}), f32[16,256,128]{2,0,1:T(8,128)}, u32[]{:S(2)}, u32[]{:S(2)}) async-start(f32[16,256,128]{2,0,1:T(8,128)} %copy.36), calls=%async_computation.2 | async-start | bytes 4194304 | tf_op jit(solution)/shard_map/all_to_all | solution.py:121
  104.2 2.5 %fusion.24 = f32[2,8,256,128]{3,1,2,0:T(8,128)S(1)} fusion(f32[2,8,256,128]{3,2,1,0:T(8,128)S(1)} %bitcast.67, f32[32768]{0:T(1024)S(1)} %subtract_bitcast_fusion), kind=kOutput, calls=%fused_computation.45 | convolution fusion | flops 101712128 | bytes 4325376 | tf_op jit(solution)/shard_map/ij,bjr->bir/dot_general | solution.py:47
  109.7 42.7 %all-to-all-done.2 = f32[16,256,128]{2,0,1:T(8,128)} async-done(((f32[16,256,128]{2,0,1:T(8,128)}), f32[16,256,128]{2,0,1:T(8,128)}, u32[]{:S(2)}, u32[]{:S(2)}) %all-to-all-start.2) | async-done | bytes 2097184 | tf_op jit(solution)/shard_map/all_to_all | solution.py:121
  152.3 3.4 %all-to-all-start.1 = ((f32[1,256,128]{2,0,1:T(1,128)}), f32[1,256,128]{2,0,1:T(1,128)S(1)}, u32[]{:S(2)}, u32[]{:S(2)}) async-start(f32[1,256,128]{2,0,1:T(1,128)} %bitcast.14), calls=%async_computation.1 | async-start | bytes 262144 | tf_op jit(solution)/shard_map/all_to_all | solution.py:102
  155.7 3.5 %copy.38 = f32[8,16,32,128]{3,2,1,0:T(8,128)} copy(f32[8,16,32,128]{3,1,2,0:T(8,128)} %bitcast.18) | data formatting | bytes 4194304 | tf_op jit(solution)/shard_map/all_to_all | solution.py:121
  159.3 3.1 %all-to-all-done.1 = f32[1,256,128]{2,0,1:T(1,128)S(1)} async-done(((f32[1,256,128]{2,0,1:T(1,128)}), f32[1,256,128]{2,0,1:T(1,128)S(1)}, u32[]{:S(2)}, u32[]{:S(2)}) %all-to-all-start.1) | async-done | bytes 131104 | tf_op jit(solution)/shard_map/all_to_all | solution.py:102
  162.4 6.9 %all-to-all-start.3 = ((f32[128,32,128]{2,1,0:T(8,128)}), f32[128,32,128]{2,1,0:T(8,128)S(1)}, u32[]{:S(2)}, u32[]{:S(2)}) async-start(f32[128,32,128]{2,1,0:T(8,128)} %bitcast.19), calls=%async_computation.3 | async-start | bytes 4194304 | tf_op jit(solution)/shard_map/all_to_all | solution.py:122
  170.6 23.3 %all-to-all-done.3 = f32[128,32,128]{2,1,0:T(8,128)S(1)} async-done(((f32[128,32,128]{2,1,0:T(8,128)}), f32[128,32,128]{2,1,0:T(8,128)S(1)}, u32[]{:S(2)}, u32[]{:S(2)}) %all-to-all-start.3) | async-done | bytes 2097184 | tf_op jit(solution)/shard_map/all_to_all | solution.py:122
  193.9 1.6 copy.51
  (56 shorter events, 18.2 us)
Async XLA Ops:
  0.6 35.5 %copy-start = (s32[256,512]{1,0:T(8,128)S(1)}, s32[256,512]{1,0:T(8,128)}, u32[]{:S(2)}) copy-start(s32[256,512]{1,0:T(8,128)} %param.12) | copy-start | bytes 1572868
  4.1 14.3 %copy-start.5 = (f32[16,256,128]{2,1,0:T(8,128)}, f32[16,256,128]{2,1,0:T(8,128)S(1)}, u32[]{:S(2)}) copy-start(f32[16,256,128]{2,1,0:T(8,128)S(1)} %get-tuple-element.36) | copy-start | bytes 6291460
  18.5 1.3 copy-start.3
  19.8 18.1 %collective-permute-start.2 = (f32[2,256,128]{2,1,0:T(8,128)S(1)}, f32[2,256,128]{2,1,0:T(8,128)S(1)}, u32[]{:S(2)}, u32[]{:S(2)}) collective-permute-start(f32[2,256,128]{2,1,0:T(8,128)S(1)} %slice.105), channel_id=1, source_target_pairs={{1,0},{2,1},{3,2},{4,3},{5,4},{6,5},{7,6},{9,8},{10,9},{11,10},{12... | collective-permute-start | bytes 786440 | tf_op jit(solution)/shard_map/ppermute | solution.py:12
  33.6 2.6 %copy-start.12 = (f32[3,16]{1,0:T(4,128)S(1)}, f32[3,16]{1,0:T(4,128)}, u32[]{:S(2)}) copy-start(f32[3,16]{1,0:T(4,128)} %param.13) | copy-start | bytes 580
  34.8 8.5 %collective-permute-start = (f32[2,256,128]{2,1,0:T(8,128)}, f32[2,256,128]{2,1,0:T(8,128)S(1)}, u32[]{:S(2)}, u32[]{:S(2)}) collective-permute-start(f32[2,256,128]{2,1,0:T(8,128)} %slice.74), channel_id=1, source_target_pairs={{1,0},{2,1},{3,2},{4,3},{5,4},{6,5},{7,6},{9,8},{10,9},{11,10},{12... | collective-permute-start | bytes 786440 | tf_op jit(solution)/shard_map/ppermute | solution.py:12
  41.7 2.5 %copy-start.6 = (f32[16,256,128]{2,1,0:T(8,128)S(1)}, f32[16,256,128]{2,1,0:T(8,128)}, u32[]{:S(2)}) copy-start(f32[16,256,128]{2,1,0:T(8,128)} %copy-done.5) | copy-start | bytes 6291460
  44.4 2.2 %copy-start.2 = (f32[18,256,128]{2,1,0:T(8,128)}, f32[18,256,128]{2,1,0:T(8,128)S(1)}, u32[]{:S(2)}) copy-start(f32[18,256,128]{2,1,0:T(8,128)S(1)} %pad_maximum_fusion) | copy-start | bytes 7077892
  50.9 11.4 %collective-permute-start.3 = (f32[18,258,1]{1,2,0:T(1,128)S(1)}, f32[18,258,1]{1,2,0:T(1,128)S(1)}, u32[]{:S(2)}, u32[]{:S(2)}) collective-permute-start(f32[18,258,1]{1,2,0:T(1,128)S(1)} %copy.33), channel_id=1, source_target_pairs={{8,0},{16,8},{24,16},{9,1},{17,9},{25,17},{10,2},{18,10},{26,18},{... | collective-permute-start | bytes 55736 | tf_op jit(solution)/shard_map/ppermute | solution.py:12
  54.9 5.3 %copy-start.7 = (f32[16,256,128]{2,1,0:T(8,128)S(1)}, f32[16,256,128]{2,1,0:T(8,128)}, u32[]{:S(2)}) copy-start(f32[16,256,128]{2,1,0:T(8,128)} %copy-done.5) | copy-start | bytes 6291460
  54.9 11.8 %collective-permute-start.1 = (f32[18,258,1]{1,2,0:T(1,128)S(1)}, f32[18,258,1]{1,2,0:T(1,128)S(1)}, u32[]{:S(2)}, u32[]{:S(2)}) collective-permute-start(f32[18,258,1]{1,2,0:T(1,128)S(1)} %copy.30), channel_id=1, source_target_pairs={{8,0},{16,8},{24,16},{9,1},{17,9},{25,17},{10,2},{18,10},{26,18},{... | collective-permute-start | bytes 55736 | tf_op jit(solution)/shard_map/ppermute | solution.py:12
  66.8 4.3 %copy-start.10 = (f32[1,256,128]{2,0,1:T(1,128)S(1)}, f32[1,256,128]{2,0,1:T(1,128)}, u32[]{:S(2)}) copy-start(f32[1,256,128]{2,0,1:T(1,128)} %get-tuple-element.40) | copy-start | bytes 393220
  66.8 4.3 %copy-start.11 = (f32[1,256,128]{2,0,1:T(1,128)S(1)}, f32[1,256,128]{2,0,1:T(1,128)}, u32[]{:S(2)}) copy-start(f32[1,256,128]{2,0,1:T(1,128)} %get-tuple-element.41) | copy-start | bytes 393220
  83.2 9.0 %copy-start.4 = (f32[16,256,128]{2,1,0:T(8,128)S(1)}, f32[16,256,128]{2,1,0:T(8,128)}, u32[]{:S(2)}) copy-start(f32[16,256,128]{2,1,0:T(8,128)} %copy-done.3) | copy-start | bytes 6291460
  85.5 13.4 %all-to-all-start = ((f32[1,256,128]{2,0,1:T(1,128)}), f32[1,256,128]{2,0,1:T(1,128)S(1)}, u32[]{:S(2)}, u32[]{:S(2)}) async-start(f32[1,256,128]{2,0,1:T(1,128)} %bitcast.7), calls=%async_computation | async-start | bytes 262144 | tf_op jit(solution)/shard_map/all_to_all | solution.py:103
  94.7 9.5 %copy-start.8 = (f32[16,256,128]{2,1,0:T(8,128)S(1)}, f32[16,256,128]{2,1,0:T(8,128)}, u32[]{:S(2)}) copy-start(f32[16,256,128]{2,1,0:T(8,128)} %get-tuple-element.38) | copy-start | bytes 6291460
  98.9 53.4 %all-to-all-start.2 = ((f32[16,256,128]{2,0,1:T(8,128)}), f32[16,256,128]{2,0,1:T(8,128)}, u32[]{:S(2)}, u32[]{:S(2)}) async-start(f32[16,256,128]{2,0,1:T(8,128)} %copy.36), calls=%async_computation.2 | async-start | bytes 4194304 | tf_op jit(solution)/shard_map/all_to_all | solution.py:121
  106.7 1.7 copy-start.9
  152.3 10.1 %all-to-all-start.1 = ((f32[1,256,128]{2,0,1:T(1,128)}), f32[1,256,128]{2,0,1:T(1,128)S(1)}, u32[]{:S(2)}, u32[]{:S(2)}) async-start(f32[1,256,128]{2,0,1:T(1,128)} %bitcast.14), calls=%async_computation.1 | async-start | bytes 262144 | tf_op jit(solution)/shard_map/all_to_all | solution.py:102
  162.4 31.5 %all-to-all-start.3 = ((f32[128,32,128]{2,1,0:T(8,128)}), f32[128,32,128]{2,1,0:T(8,128)S(1)}, u32[]{:S(2)}, u32[]{:S(2)}) async-start(f32[128,32,128]{2,1,0:T(8,128)} %bitcast.19), calls=%async_computation.3 | async-start | bytes 4194304 | tf_op jit(solution)/shard_map/all_to_all | solution.py:122
  169.4 26.2 %copy-start.1 = (s32[256,512]{1,0:T(8,128)S(1)}, s32[256,512]{1,0:T(8,128)}, u32[]{:S(2)}) copy-start(s32[256,512]{1,0:T(8,128)} %param.12) | copy-start | bytes 1572868
where the time goes:
time: 197 us; the launch traced here: 196 us
  waiting for transfers between devices  73.3 us (37%)
  local copies, waits for them, and re-layouts  47.3 us (24%)
  other arithmetic  30.4 us (15%)
  starting transfers between devices  26.8 us (14%)
  blocking collectives  9.72 us (5%)
  matrix products  7 us (4%)
    all_to_all x1, waiting for transfers between devices, local(): lax.all_to_all(lit, 'screen', split_axis=1, concat_axis=0, tiled=True)  42.7 us
    all_to_all x1, waiting for transfers between devices, local(): lax.all_to_all(lit_cam, 'light', split_axis=0, concat_axis=2, tiled=True)  23.3 us
    add x1, other arithmetic, resample(): mixed = near + light_w * (further - near)  12 us
    reshape x1, local copies, waits for them, and re-layouts, local(): density.reshape(bricks_b, BRICK, bricks_a, BRICK, bricks_l, BRICK)  10.6 us
    all_gather x1, blocking collectives, carried_in(): gathered = lax.all_gather(part, axis)  9.72 us
    slice x4, local copies, waits for them, and re-layouts, march_slabs(): tails = passed_along((dens_ext[:, :, :1], lit_ext[:, :, :1]), 'light', -1)  8.64 us
    all_to_all x1, starting transfers between devices, local(): lax.all_to_all(lit_cam, 'light', split_axis=0, concat_axis=2, tiled=True)  6.94 us
    all_to_all x1, starting transfers between devices, march_slabs(): lax.all_to_all(total[None], 'screen', split_axis=1, concat_axis=0, tiled=...  6.67 us
  transfers between devices with their start and end apart: 8, of which 4 were waited for; matrix products, arithmetic and copies ran while one was open for 24% of the time, Pallas kernels for 0%

commit v1 on v0

--- a/solution.py
+++ b/solution.py
@@ -4,6 +4,28 @@
 from jax.sharding import PartitionSpec as P
 
 BRICK = 16
+
+
+def in_blocks(shard, dim, peers):
+    before, after = (shard.shape[:dim], shard.shape[dim + 1 :])
+    return jnp.moveaxis(shard.reshape(*before, peers, -1, *after), dim, 0)
+
+
+def in_order(parts, dim):
+    shape = list(parts.shape[1:])
+    shape[dim] *= parts.shape[0]
+    return jnp.moveaxis(parts, 0, dim).reshape(shape)
+
+
+def sent_to_each(shard, axis, split_dim, concat_dim):
+    size, index = (lax.axis_size(axis), lax.axis_index(axis))
+    blocks = in_blocks(shard, split_dim, size)
+    gathered = [blocks[index]]
+    for turn in range(1, size):
+        sent = blocks[(index + turn) % size]
+        gathered.append(lax.ppermute(sent, axis, [(i, (i + turn) % size) for i in range(size)]))
+    blocks = jnp.stack(gathered)[(index - jnp.arange(size)) % size]
+    return in_order(blocks, concat_dim)
 
 
 def passed_along(value, axis, by):
@@ -118,7 +140,7 @@
     before = carried_in(totals, "light", jnp.add, jnp.zeros_like(totals))
     incoming = lax.dynamic_slice_in_dim(light_in, screen_idx * slab_b, slab_b, 0)
     lit = albedo * incoming[:, :, None] * jnp.exp(-(local_depth + before[:, :, None]))
-    lit_cam = lax.all_to_all(lit, "screen", split_axis=1, concat_axis=0, tiled=True)
+    lit_cam = sent_to_each(lit, "screen", 1, 0)
     lit_cam = lax.all_to_all(lit_cam, "light", split_axis=0, concat_axis=2, tiled=True)
     picture, passing = march_slabs(masked, lit, phase, fractions)
     return (picture, passing, lit_cam)

time: 197 us -> 177 us (0.90)
  waiting for transfers between devices: 73.3 us -> 36.3 us
  local copies, waits for them, and re-layouts: 47.3 us -> 60.7 us
  starting transfers between devices: 26.8 us -> 34.4 us
  other arithmetic: 30.4 us -> 27.2 us
    all_to_all x1 -> x0, waiting for transfers between devices: 42.7 us -> none  [local(): lax.all_to_all(lit, 'screen', split_axis=1, concat_axis=0, tiled=True)]
    ppermute x0 -> x7, starting transfers between devices: none -> 14 us  [sent_to_each(): lax.ppermute(sent, axis, [(i, (i + turn) % size) for i in range(size)])]
    ppermute x0 -> x7, waiting for transfers between devices: none -> 10.3 us  [sent_to_each(): lax.ppermute(sent, axis, [(i, (i + turn) % size) for i in range(size)])]
    unnamed x27 -> x30, local copies, waits for them, and re-layouts: 3.87 us -> 10.7 us
    all_to_all x1 -> x0, starting transfers between devices: 4.36 us -> none  [local(): lax.all_to_all(lit, 'screen', split_axis=1, concat_axis=0, tiled=True)]
    gather x0 -> x1, local copies, waits for them, and re-layouts: none -> 3.59 us  [sent_to_each(): blocks = jnp.stack(gathered)[(index - jnp.arange(size)) % size]]
    all_to_all x1 -> x0, local copies, waits for them, and re-layouts: 3.54 us -> none  [local(): lax.all_to_all(lit, 'screen', split_axis=1, concat_axis=0, tiled=True)]
    all_to_all x1, waiting for transfers between devices: 4.2 us -> 1.28 us  [march_slabs(): lax.all_to_all(total[None], 'screen', split_axis=1, concat_axis=0, tiled=...]
  transfers between devices with their start and end apart: 8 -> 14, of which waited for: 4 -> 5; matrix products, arithmetic and copies ran while one was open for 24% -> 46% of each run, Pallas kernels for 0% -> 0%
where the time goes in v1:
time: 177 us; the launch traced here: 176 us
  local copies, waits for them, and re-layouts  60.7 us (34%)
  waiting for transfers between devices  36.3 us (21%)
  starting transfers between devices  34.4 us (19%)
  other arithmetic  27.2 us (15%)
  blocking collectives  9.71 us (5%)
  matrix products  6.73 us (4%)
    all_to_all x1, waiting for transfers between devices, local(): lax.all_to_all(lit_cam, 'light', split_axis=0, concat_axis=2, tiled=True)  23.3 us
    ppermute x7, starting transfers between devices, sent_to_each(): lax.ppermute(sent, axis, [(i, (i + turn) % size) for i in range(size)])  14 us
    add x1, other arithmetic, resample(): mixed = near + light_w * (further - near)  12 us
    unnamed x30, local copies, waits for them, and re-layouts  10.7 us
    reshape x1, local copies, waits for them, and re-layouts, local(): density.reshape(bricks_b, BRICK, bricks_a, BRICK, bricks_l, BRICK)  10.5 us
    ppermute x7, waiting for transfers between devices, sent_to_each(): lax.ppermute(sent, axis, [(i, (i + turn) % size) for i in range(size)])  10.3 us
    slice x4, local copies, waits for them, and re-layouts, march_slabs(): tails = passed_along((dens_ext[:, :, :1], lit_ext[:, :, :1]), 'light', -1)  9.92 us
    all_gather x1, blocking collectives, carried_in(): gathered = lax.all_gather(part, axis)  9.71 us
  transfers between devices with their start and end apart: 14, of which 5 were waited for; matrix products, arithmetic and copies ran while one was open for 46% of the time, Pallas kernels for 0%

profile of v1, /device:TPU:0, one launch (start us, length us, event | category | flops | bytes accessed | tf_op | source)
XLA Modules:
  0.0 176.1 jit_solution(16131449961681536945)
XLA Ops:
  4.2 1.8 %fusion.37 = (f32[16,256]{1,0:T(8,128)S(1)}, f32[16,256,128]{2,1,0:T(8,128)}) fusion(f32[16,256,128]{2,1,0:T(8,128)S(1)} %copy-done.8, f32[256,128]{1,0:T(8,128)S(1)} %mul.121), kind=kLoop, calls=%fused_computation.85 | loop fusion | flops 1044480 | bytes 4341760 | tf_op jit(solution)/shard_map/reduce_sum | solution.py:57
  6.0 9.7 %all-gather = f32[64,256]{1,0:T(8,128)S(1)} all-gather(f32[16,256]{1,0:T(8,128)S(1)} %get-tuple-element.35), channel_id=2, replica_groups=mesh['light'=4,'screen'=8] {'light'}, dimensions={0}, use_global_device_ids=true | all-gather | bytes 81920 | tf_op jit(solution)/shard_map/all_gather | solution.py:39
  16.5 3.6 %exponential_multiply_fusion = f32[16,256,128]{2,1,0:T(8,128)S(1)} fusion(f32[16,256,128]{2,1,0:T(8,128)} %param.9, f32[16,256,128]{2,1,0:T(8,128)} %get-tuple-element.36, f32[16,256]{1,0:T(8,128)S(1)} %get-tuple-element.26, f32[16,256]{1,0:T(8,128)S(1)} %sub.79, f32[16,256]{1,0:T(8,128)S(1)} %constant_dynamic-slice_fusion), kind=kOutput, calls=%fused_computation.43 | convolution fusion | flops 807944192 | bytes 6340608 | tf_op jit(solution)/shard_map/dot_general | solution.py:56
  23.5 4.3 %collective-permute-start.10 = (f32[16,32,128]{2,1,0:T(8,128)}, f32[16,32,128]{2,1,0:T(8,128)}, u32[]{:S(2)}, u32[]{:S(2)}) collective-permute-start(f32[16,32,128]{2,1,0:T(8,128)} %get-tuple-element.39), channel_id=1, source_target_pairs={{0,7},{1,0},{2,1},{3,2},{4,3},{5,4},{6,5},{7,6},{8,15},{9,8},{10,9... | collective-permute-start | bytes 786440 | tf_op jit(solution)/shard_map/ppermute | solution.py:26
  28.9 10.5 %reshape.152 = f32[1,16,16,16,8,16]{5,4,3,2,1,0:T(8,128)} reshape(f32[16,256,128]{2,1,0:T(8,128)} %param.8) | data formatting | bytes 4194304 | tf_op jit(solution)/shard_map/reshape | solution.py:134
  40.2 1.9 %slice_multiply_fusion = f32[1,2,16,16,8,16]{5,4,3,2,1,0:T(8,128)S(1)} fusion(f32[1,16,16,16,8,16]{5,4,3,2,1,0:T(8,128)} %reshape.152, f32[16,8]{1,0:T(8,128)S(1)} %copy.16), kind=kLoop, calls=%fused_computation.42 | loop fusion | flops 65536 | bytes 524800 | tf_op jit(solution)/shard_map/mul | solution.py:134
  45.7 1.7 pad_maximum_fusion.1
  49.1 4.2 %collective-permute-start.5 = (f32[16,32,128]{2,1,0:T(8,128)S(1)}, f32[16,32,128]{2,1,0:T(8,128)S(1)}, u32[]{:S(2)}, u32[]{:S(2)}) collective-permute-start(f32[16,32,128]{2,1,0:T(8,128)S(1)} %copy-done.9), channel_id=1, source_target_pairs={{0,2},{1,3},{2,4},{3,5},{4,6},{5,7},{6,0},{7,1},{8,10},{9,11},{10,... | collective-permute-start | bytes 786440 | tf_op jit(solution)/shard_map/ppermute | solution.py:26
  56.7 2.9 %collective-permute-done.5 = f32[16,32,128]{2,1,0:T(8,128)S(1)} collective-permute-done((f32[16,32,128]{2,1,0:T(8,128)S(1)}, f32[16,32,128]{2,1,0:T(8,128)S(1)}, u32[]{:S(2)}, u32[]{:S(2)}) %collective-permute-start.5) | collective-permute-done | bytes 262176 | tf_op jit(solution)/shard_map/ppermute | solution.py:26
  59.6 3.0 %collective-permute-start.6 = (f32[16,32,128]{2,1,0:T(8,128)}, f32[16,32,128]{2,1,0:T(8,128)}, u32[]{:S(2)}, u32[]{:S(2)}) collective-permute-start(f32[16,32,128]{2,1,0:T(8,128)} %get-tuple-element.43), channel_id=1, source_target_pairs={{0,3},{1,4},{2,5},{3,6},{4,7},{5,0},{6,1},{7,2},{8,11},{9,12},{10,... | collective-permute-start | bytes 786440 | tf_op jit(solution)/shard_map/ppermute | solution.py:26
  64.9 2.2 %pad_slice_fusion.2 = f32[18,256,127]{2,1,0:T(8,128)} fusion(f32[18,256,128]{2,1,0:T(8,128)S(1)} %pad_maximum_fusion.1), kind=kLoop, calls=%fused_computation.26 | loop fusion | bytes 4700160 | tf_op jit(solution)/shard_map/slice | solution.py:87
  67.1 3.3 %copy.21 = f32[18,258,1]{1,2,0:T(1,128)} copy(f32[18,258,1]{2,1,0:T(8,128)} %pad_slice_fusion.3) | data formatting | bytes 37152 | tf_op jit(solution)/shard_map/slice | solution.py:117
  70.4 3.3 %copy.18 = f32[18,258,1]{1,2,0:T(1,128)} copy(f32[18,258,1]{2,1,0:T(8,128)} %pad_slice_fusion.5) | data formatting | bytes 37152 | tf_op jit(solution)/shard_map/slice | solution.py:117
  73.7 7.4 %collective-permute-done.6 = f32[16,32,128]{2,1,0:T(8,128)} collective-permute-done((f32[16,32,128]{2,1,0:T(8,128)}, f32[16,32,128]{2,1,0:T(8,128)}, u32[]{:S(2)}, u32[]{:S(2)}) %collective-permute-start.6) | collective-permute-done | bytes 262176 | tf_op jit(solution)/shard_map/ppermute | solution.py:26
  82.4 1.7 bitcast_dynamic-update-slice_fusion.4
  86.3 3.9 %pad_slice_fusion.4 = f32[18,256,127]{2,1,0:T(8,128)} fusion(f32[18,256,128]{2,1,0:T(8,128)} %copy-done.2), kind=kLoop, calls=%fused_computation.28 | loop fusion | bytes 4700160 | tf_op jit(solution)/shard_map/slice | solution.py:87
  90.2 2.1 %fusion.3 = f32[18,256,127]{2,1,0:T(8,128)} fusion(f32[2,256,128]{2,1,0:T(8,128)S(1)} %collective-permute-done.2, f32[16,256,128]{2,1,0:T(8,128)S(1)} %copy-done.4), kind=kLoop, calls=%fused_computation.10 | loop fusion | flops 585216 | bytes 4700160 | tf_op jit(solution)/shard_map/concatenate | solution.py:116
  92.3 1.7 bitcast_dynamic-update-slice_fusion.2
  94.0 1.7 bitcast_dynamic-update-slice_fusion.1
  95.7 2.1 %fusion.4 = f32[18,256,127]{2,1,0:T(8,128)} fusion(f32[2,256,128]{2,1,0:T(8,128)S(1)} %collective-permute-done, f32[16,256,128]{2,1,0:T(8,128)S(1)} %copy-done.6), kind=kLoop, calls=%fused_computation.11 | loop fusion | flops 585216 | bytes 4700160 | tf_op jit(solution)/shard_map/concatenate | solution.py:115
  97.9 2.1 %copy.23 = f32[18,256,1]{2,1,0:T(8,128)} copy(f32[18,256,1]{1,2,0:T(1,128)S(1)} %get-tuple-element.51) | data formatting | bytes 36864 | tf_op jit(solution)/shard_map/slice | solution.py:85
  100.0 2.2 %copy.22 = f32[18,256,1]{2,1,0:T(8,128)} copy(f32[18,256,1]{1,2,0:T(1,128)S(1)} %get-tuple-element.52) | data formatting | bytes 36864 | tf_op jit(solution)/shard_map/slice | solution.py:84
  103.1 2.1 %copy.20 = f32[18,256,1]{2,1,0:T(8,128)} copy(f32[18,256,1]{1,2,0:T(1,128)S(1)} %get-tuple-element.53) | data formatting | bytes 36864 | tf_op jit(solution)/shard_map/slice | solution.py:85
  105.2 2.1 %copy.19 = f32[18,256,1]{2,1,0:T(8,128)} copy(f32[18,256,1]{1,2,0:T(1,128)S(1)} %get-tuple-element.54) | data formatting | bytes 36864 | tf_op jit(solution)/shard_map/slice | solution.py:84
  107.3 12.0 %fusion.14 = (f32[18,256,128]{2,1,0:T(8,128)}, f32[18,256,128]{2,1,0:T(8,128)S(1)}) fusion(f32[18,256,1]{2,1,0:T(8,128)} %copy.22, f32[18,256,127]{2,1,0:T(8,128)} %fusion.3, f32[18,256,1]{2,1,0:T(8,128)} %copy.23, f32[18,256,127]{2,1,0:T(8,128)} %pad_slice_fusion.2, f32[18,256,128]{2,1,0:T(8,128)S(1)} %pad_maximum_fusion.1, f32[256,128]{1,0:T(8,128)S(1)} %bitcast.106, ...), kind=kLoop, calls=%fused_computation.25 | loop fusion | flops 12976128 | bytes 19136512 | tf_op jit(solution)/shard_map/add | solution.py:93
  121.3 3.9 %all-to-all-start = ((f32[1,256,128]{2,0,1:T(1,128)}), f32[1,256,128]{2,0,1:T(1,128)S(1)}, u32[]{:S(2)}, u32[]{:S(2)}) async-start(f32[1,256,128]{2,0,1:T(1,128)} %bitcast.7), calls=%async_computation | async-start | bytes 262144 | tf_op jit(solution)/shard_map/all_to_all | solution.py:125
  125.3 2.5 %fusion.24 = f32[2,8,256,128]{3,1,2,0:T(8,128)S(1)} fusion(f32[2,8,256,128]{3,2,1,0:T(8,128)S(1)} %bitcast.99, f32[32768]{0:T(1024)S(1)} %subtract_bitcast_fusion), kind=kOutput, calls=%fused_computation.46 | convolution fusion | flops 101712128 | bytes 4325376 | tf_op jit(solution)/shard_map/ij,bjr->bir/dot_general | solution.py:69
  132.0 3.8 %all-to-all-start.1 = ((f32[1,256,128]{2,0,1:T(1,128)}), f32[1,256,128]{2,0,1:T(1,128)S(1)}, u32[]{:S(2)}, u32[]{:S(2)}) async-start(f32[1,256,128]{2,0,1:T(1,128)} %bitcast.14), calls=%async_computation.1 | async-start | bytes 262144 | tf_op jit(solution)/shard_map/all_to_all | solution.py:124
  135.8 1.7 bitcast_dynamic-update-slice_fusion
  137.5 3.6 %gather_fusion = f32[8,16,32,128]{3,2,1,0:T(8,128)} fusion(f32[8,16,32,128]{3,2,1,0:T(8,128)} %bitcast_dynamic-update-slice_fusion, s32[1024]{0:T(1024)S(1)} %pad_clamp_fusion), kind=kCustom, calls=%fused_computation | custom fusion | bytes 4194336 | tf_op jit(solution)/shard_map/gather | solution.py:27
  142.6 7.4 %all-to-all-start.2 = ((f32[128,32,128]{2,1,0:T(8,128)}), f32[128,32,128]{2,1,0:T(8,128)S(1)}, u32[]{:S(2)}, u32[]{:S(2)}) async-start(f32[128,32,128]{2,1,0:T(8,128)} %bitcast.33), calls=%async_computation.2 | async-start | bytes 4194304 | tf_op jit(solution)/shard_map/all_to_all | solution.py:144
  151.2 23.3 %all-to-all-done.2 = f32[128,32,128]{2,1,0:T(8,128)S(1)} async-done(((f32[128,32,128]{2,1,0:T(8,128)}), f32[128,32,128]{2,1,0:T(8,128)S(1)}, u32[]{:S(2)}, u32[]{:S(2)}) %all-to-all-start.2) | async-done | bytes 2097184 | tf_op jit(solution)/shard_map/all_to_all | solution.py:144
  (74 shorter events, 35.5 us)
Async XLA Ops:
  0.6 41.4 %copy-start = (s32[256,512]{1,0:T(8,128)S(1)}, s32[256,512]{1,0:T(8,128)}, u32[]{:S(2)}) copy-start(s32[256,512]{1,0:T(8,128)} %param.12) | copy-start | bytes 1572868
  0.6 3.6 %copy-start.8 = (f32[16,256,128]{2,1,0:T(8,128)S(1)}, f32[16,256,128]{2,1,0:T(8,128)}, u32[]{:S(2)}) copy-start(f32[16,256,128]{2,1,0:T(8,128)} %param.8) | copy-start | bytes 6291460
  20.1 19.4 %copy-start.3 = (f32[16,256,128]{2,1,0:T(8,128)}, f32[16,256,128]{2,1,0:T(8,128)S(1)}, u32[]{:S(2)}) copy-start(f32[16,256,128]{2,1,0:T(8,128)S(1)} %exponential_multiply_fusion) | copy-start | bytes 6291460
  20.8 23.6 %collective-permute-start.2 = (f32[2,256,128]{2,1,0:T(8,128)}, f32[2,256,128]{2,1,0:T(8,128)S(1)}, u32[]{:S(2)}, u32[]{:S(2)}) collective-permute-start(f32[2,256,128]{2,1,0:T(8,128)} %slice.107), channel_id=1, source_target_pairs={{1,0},{2,1},{3,2},{4,3},{5,4},{6,5},{7,6},{9,8},{10,9},{11,10},{12... | collective-permute-start | bytes 786440 | tf_op jit(solution)/shard_map/ppermute | solution.py:34
  23.5 112.3 %collective-permute-start.10 = (f32[16,32,128]{2,1,0:T(8,128)}, f32[16,32,128]{2,1,0:T(8,128)}, u32[]{:S(2)}, u32[]{:S(2)}) collective-permute-start(f32[16,32,128]{2,1,0:T(8,128)} %get-tuple-element.39), channel_id=1, source_target_pairs={{0,7},{1,0},{2,1},{3,2},{4,3},{5,4},{6,5},{7,6},{8,15},{9,8},{10,9... | collective-permute-start | bytes 786440 | tf_op jit(solution)/shard_map/ppermute | solution.py:26
  27.9 66.1 %collective-permute-start.9 = (f32[16,32,128]{2,1,0:T(8,128)}, f32[16,32,128]{2,1,0:T(8,128)}, u32[]{:S(2)}, u32[]{:S(2)}) collective-permute-start(f32[16,32,128]{2,1,0:T(8,128)} %get-tuple-element.40), channel_id=1, source_target_pairs={{0,6},{1,7},{2,0},{3,1},{4,2},{5,3},{6,4},{7,5},{8,14},{9,15},{10,... | collective-permute-start | bytes 786440 | tf_op jit(solution)/shard_map/ppermute | solution.py:26
  28.3 64.0 %collective-permute-start.8 = (f32[16,32,128]{2,1,0:T(8,128)}, f32[16,32,128]{2,1,0:T(8,128)}, u32[]{:S(2)}, u32[]{:S(2)}) collective-permute-start(f32[16,32,128]{2,1,0:T(8,128)} %get-tuple-element.41), channel_id=1, source_target_pairs={{0,5},{1,6},{2,7},{3,0},{4,1},{5,2},{6,3},{7,4},{8,13},{9,14},{10,... | collective-permute-start | bytes 786440 | tf_op jit(solution)/shard_map/ppermute | solution.py:26
  28.3 25.2 %collective-permute-start.4 = (f32[16,32,128]{2,1,0:T(8,128)}, f32[16,32,128]{2,1,0:T(8,128)}, u32[]{:S(2)}, u32[]{:S(2)}) collective-permute-start(f32[16,32,128]{2,1,0:T(8,128)} %get-tuple-element.45), channel_id=1, source_target_pairs={{0,1},{1,2},{2,3},{3,4},{4,5},{5,6},{6,7},{7,0},{8,9},{9,10},{10,1... | collective-permute-start | bytes 786440 | tf_op jit(solution)/shard_map/ppermute | solution.py:26
  40.2 1.9 %copy-start.10 = (f32[3,16]{1,0:T(4,128)S(1)}, f32[3,16]{1,0:T(4,128)}, u32[]{:S(2)}) copy-start(f32[3,16]{1,0:T(4,128)} %param.13) | copy-start | bytes 580
  44.4 4.7 %collective-permute-start = (f32[2,256,128]{2,1,0:T(8,128)}, f32[2,256,128]{2,1,0:T(8,128)S(1)}, u32[]{:S(2)}, u32[]{:S(2)}) collective-permute-start(f32[2,256,128]{2,1,0:T(8,128)} %slice.74), channel_id=1, source_target_pairs={{1,0},{2,1},{3,2},{4,3},{5,4},{6,5},{7,6},{9,8},{10,9},{11,10},{12... | collective-permute-start | bytes 786440 | tf_op jit(solution)/shard_map/ppermute | solution.py:34
  47.4 1.7 copy-start.9
  47.4 5.8 %copy-start.5 = (f32[16,256,128]{2,1,0:T(8,128)S(1)}, f32[16,256,128]{2,1,0:T(8,128)}, u32[]{:S(2)}) copy-start(f32[16,256,128]{2,1,0:T(8,128)} %get-tuple-element.36) | copy-start | bytes 6291460
  49.1 10.5 %collective-permute-start.5 = (f32[16,32,128]{2,1,0:T(8,128)S(1)}, f32[16,32,128]{2,1,0:T(8,128)S(1)}, u32[]{:S(2)}, u32[]{:S(2)}) collective-permute-start(f32[16,32,128]{2,1,0:T(8,128)S(1)} %copy-done.9), channel_id=1, source_target_pairs={{0,2},{1,3},{2,4},{3,5},{4,6},{5,7},{6,0},{7,1},{8,10},{9,11},{10,... | collective-permute-start | bytes 786440 | tf_op jit(solution)/shard_map/ppermute | solution.py:26
  53.5 11.4 %copy-start.2 = (f32[18,256,128]{2,1,0:T(8,128)}, f32[18,256,128]{2,1,0:T(8,128)S(1)}, u32[]{:S(2)}) copy-start(f32[18,256,128]{2,1,0:T(8,128)S(1)} %pad_maximum_fusion) | copy-start | bytes 7077892
  53.5 30.6 %collective-permute-start.7 = (f32[16,32,128]{2,1,0:T(8,128)}, f32[16,32,128]{2,1,0:T(8,128)S(1)}, u32[]{:S(2)}, u32[]{:S(2)}) collective-permute-start(f32[16,32,128]{2,1,0:T(8,128)} %get-tuple-element.42), channel_id=1, source_target_pairs={{0,4},{1,5},{2,6},{3,7},{4,0},{5,1},{6,2},{7,3},{8,12},{9,13},{10,... | collective-permute-start | bytes 786440 | tf_op jit(solution)/shard_map/ppermute | solution.py:26
  59.6 21.5 %collective-permute-start.6 = (f32[16,32,128]{2,1,0:T(8,128)}, f32[16,32,128]{2,1,0:T(8,128)}, u32[]{:S(2)}, u32[]{:S(2)}) collective-permute-start(f32[16,32,128]{2,1,0:T(8,128)} %get-tuple-element.43), channel_id=1, source_target_pairs={{0,3},{1,4},{2,5},{3,6},{4,7},{5,0},{6,1},{7,2},{8,11},{9,12},{10,... | collective-permute-start | bytes 786440 | tf_op jit(solution)/shard_map/ppermute | solution.py:26
  81.1 16.7 %collective-permute-start.3 = (f32[18,258,1]{1,2,0:T(1,128)}, f32[18,258,1]{1,2,0:T(1,128)S(1)}, u32[]{:S(2)}, u32[]{:S(2)}) collective-permute-start(f32[18,258,1]{1,2,0:T(1,128)} %copy.21), channel_id=1, source_target_pairs={{8,0},{16,8},{24,16},{9,1},{17,9},{25,17},{10,2},{18,10},{26,18},{... | collective-permute-start | bytes 55736 | tf_op jit(solution)/shard_map/ppermute | solution.py:34
  84.1 18.1 %collective-permute-start.1 = (f32[18,258,1]{1,2,0:T(1,128)}, f32[18,258,1]{1,2,0:T(1,128)}, u32[]{:S(2)}, u32[]{:S(2)}) collective-permute-start(f32[18,258,1]{1,2,0:T(1,128)} %copy.18), channel_id=1, source_target_pairs={{8,0},{16,8},{24,16},{9,1},{17,9},{25,17},{10,2},{18,10},{26,18},{... | collective-permute-start | bytes 55736 | tf_op jit(solution)/shard_map/ppermute | solution.py:34
  86.3 3.9 %copy-start.4 = (f32[16,256,128]{2,1,0:T(8,128)S(1)}, f32[16,256,128]{2,1,0:T(8,128)}, u32[]{:S(2)}) copy-start(f32[16,256,128]{2,1,0:T(8,128)} %copy-done.3) | copy-start | bytes 6291460
  90.2 5.5 %copy-start.6 = (f32[16,256,128]{2,1,0:T(8,128)S(1)}, f32[16,256,128]{2,1,0:T(8,128)}, u32[]{:S(2)}) copy-start(f32[16,256,128]{2,1,0:T(8,128)} %get-tuple-element.36) | copy-start | bytes 6291460
  121.3 10.7 %all-to-all-start = ((f32[1,256,128]{2,0,1:T(1,128)}), f32[1,256,128]{2,0,1:T(1,128)S(1)}, u32[]{:S(2)}, u32[]{:S(2)}) async-start(f32[1,256,128]{2,0,1:T(1,128)} %bitcast.7), calls=%async_computation | async-start | bytes 262144 | tf_op jit(solution)/shard_map/all_to_all | solution.py:125
  127.7 1.7 copy-start.7
  132.0 10.6 %all-to-all-start.1 = ((f32[1,256,128]{2,0,1:T(1,128)}), f32[1,256,128]{2,0,1:T(1,128)S(1)}, u32[]{:S(2)}, u32[]{:S(2)}) async-start(f32[1,256,128]{2,0,1:T(1,128)} %bitcast.14), calls=%async_computation.1 | async-start | bytes 262144 | tf_op jit(solution)/shard_map/all_to_all | solution.py:124
  142.6 31.9 %all-to-all-start.2 = ((f32[128,32,128]{2,1,0:T(8,128)}), f32[128,32,128]{2,1,0:T(8,128)S(1)}, u32[]{:S(2)}, u32[]{:S(2)}) async-start(f32[128,32,128]{2,1,0:T(8,128)} %bitcast.33), calls=%async_computation.2 | async-start | bytes 4194304 | tf_op jit(solution)/shard_map/all_to_all | solution.py:144
  174.5 1.6 copy-start.1
